TPU v7x, 32 devices: a 4x4x1 block of a 4x4x8 slice. The times are simulated.
32 devices in a mesh: batch: 1 (over z), row: 4 (over y), col: 8 (over x, core).
Axes of the slice: x: 4, y: 4, z: 1, core: 2. Of those that a mesh axis runs over, the one named last changes fastest.
The devices are a block of a 4x4x8 slice.
Arguments:
- tri_mat: bfloat16 [12288, 12288], P(('batch', 'row'), 'col')
- rhs_mat: bfloat16 [12288, 16384], P(('batch', 'row'), 'col')
Outputs:
- output: bfloat16 [12288, 16384], P(('batch', 'row'), 'col')
All inputs are finite; a program needn't handle non-finite values.
Results may differ from a plain program's by a relative error of at most 0.001.
Values are sent between devices in bfloat16 or wider.
A program may use at most 768 MiB of HBM per device.

v0:
```python
import jax
import jax.numpy as jnp
from jax import lax
from jax.sharding import PartitionSpec as P

BLOCK_SIZE = 256


def solution(mesh):
    grid_rows = mesh.shape["row"]
    grid_cols = mesh.shape["col"]
    span = max(grid_rows, grid_cols)
    row_group = span // grid_rows * BLOCK_SIZE
    col_group = span // grid_cols * BLOCK_SIZE

    def local_trmm(tri_loc, rhs_loc):
        rows_loc = tri_loc.shape[0]
        cols_loc = rhs_loc.shape[1]
        num_steps = rows_loc // row_group
        finished = []
        running = None
        for step in range(num_steps):
            l_panel = tri_loc[step * row_group:, step * col_group:(step + 1) * col_group]
            b_panel = rhs_loc[step * row_group:(step + 1) * row_group]
            l_all = lax.all_gather(l_panel, "col")
            b_all = lax.all_gather(b_panel, "row")
            l_all = l_all.reshape(grid_cols, rows_loc - step * row_group, span // grid_cols, BLOCK_SIZE)
            b_all = b_all.reshape(grid_rows, span // grid_rows, BLOCK_SIZE, cols_loc).transpose(1, 0, 2, 3)
            b_all = b_all.reshape(span // grid_cols, grid_cols, BLOCK_SIZE, cols_loc)
            update = jnp.einsum("qrjc,jqcm->rm", l_all, b_all, preferred_element_type=jnp.float32)
            running = update if running is None else running + update
            finished.append(running[:row_group].astype(jnp.bfloat16))
            running = running[row_group:]
        return jnp.concatenate(finished, axis=0)

    part_spec = P(("batch", "row"), "col")
    return jax.shard_map(local_trmm, mesh=mesh, in_specs=(part_spec, part_spec), out_specs=part_spec, check_vma=False)
```

profile of v0, /device:TPU:97, one launch (start us, length us, event | category | flops | bytes accessed | tf_op | source)
XLA Modules:
  0.0 804.0 jit_solution(4427875627294282951)
XLA Ops:
  6.6 9.2 %fusion.7 = (bf16[512,2048]{1,0:T(8,128)(2,1)}, bf16[512,2048]{1,0:T(8,128)(2,1)}, bf16[512,2048]{1,0:T(8,128)(2,1)}, bf16[512,2048]{1,0:T(8,128)(2,1)}, bf16[51...) fusion(bf16[3072,2048]{1,0:T(8,128)(2,1)} %param.3), kind=kLoop, calls=%fused_computation.18 | loop fusion | bytes 25165824 | tf_op jit(solution)/shard_map/slice | solution.py:24
  19.4 2.7 slice.71
  22.3 2.5 slice.75
  24.9 2.3 slice.79
  33.3 67.2 %all-gather.27.cloned.1.call-done = bf16[2048,2048]{1,0:T(8,128)(2,1)} async-done(((bf16[512,2048]{1,0:T(8,128)(2,1)}), bf16[2048,2048]{1,0:T(8,128)(2,1)}) %all-gather.27.cloned.1.call-update) | async-done | bytes 8388624 | tf_op jit(solution)/shard_map/all_gather | solution.py:26
  100.5 8.4 %copy.3 = bf16[4,2,256,2048]{3,2,0,1:T(8,128)(2,1)} copy(bf16[4,2,256,2048]{3,2,1,0:T(8,128)(2,1)} %bitcast.56) | data formatting | bytes 16777216 | tf_op jit(solution)/shard_map/reshape | solution.py:28
  108.9 74.9 %all-gather.31.cloned.1.call-done = bf16[2048,2048]{1,0:T(8,128)(2,1)} async-done(((bf16[512,2048]{1,0:T(8,128)(2,1)}), bf16[2048,2048]{1,0:T(8,128)(2,1)}) %all-gather.31.cloned.1.call-update) | async-done | bytes 8388624 | tf_op jit(solution)/shard_map/all_gather | solution.py:26
  183.8 8.2 %copy.4 = bf16[4,2,256,2048]{3,2,0,1:T(8,128)(2,1)} copy(bf16[4,2,256,2048]{3,2,1,0:T(8,128)(2,1)} %bitcast.57) | data formatting | bytes 16777216 | tf_op jit(solution)/shard_map/reshape | solution.py:28
  192.1 75.1 %all-gather.35.cloned.1.call-done = bf16[2048,2048]{1,0:T(8,128)(2,1)} async-done(((bf16[512,2048]{1,0:T(8,128)(2,1)}), bf16[2048,2048]{1,0:T(8,128)(2,1)}) %all-gather.35.cloned.1.call-update) | async-done | bytes 8388624 | tf_op jit(solution)/shard_map/all_gather | solution.py:26
  267.1 8.4 %copy.5 = bf16[4,2,256,2048]{3,2,0,1:T(8,128)(2,1)} copy(bf16[4,2,256,2048]{3,2,1,0:T(8,128)(2,1)} %bitcast.58) | data formatting | bytes 16777216 | tf_op jit(solution)/shard_map/reshape | solution.py:28
  275.6 74.7 %all-gather.39.cloned.1.call-done = bf16[2048,2048]{1,0:T(8,128)(2,1)} async-done(((bf16[512,2048]{1,0:T(8,128)(2,1)}), bf16[2048,2048]{1,0:T(8,128)(2,1)}) %all-gather.39.cloned.1.call-update) | async-done | bytes 8388624 | tf_op jit(solution)/shard_map/all_gather | solution.py:26
  350.3 8.3 %copy.6 = bf16[4,2,256,2048]{3,2,0,1:T(8,128)(2,1)} copy(bf16[4,2,256,2048]{3,2,1,0:T(8,128)(2,1)} %bitcast.59) | data formatting | bytes 16777216 | tf_op jit(solution)/shard_map/reshape | solution.py:28
  358.6 74.8 %all-gather.43.cloned.1.call-done = bf16[2048,2048]{1,0:T(8,128)(2,1)} async-done(((bf16[512,2048]{1,0:T(8,128)(2,1)}), bf16[2048,2048]{1,0:T(8,128)(2,1)}) %all-gather.43.cloned.1.call-update) | async-done | bytes 8388624 | tf_op jit(solution)/shard_map/all_gather | solution.py:26
  433.5 8.4 %copy.7 = bf16[4,2,256,2048]{3,2,0,1:T(8,128)(2,1)} copy(bf16[4,2,256,2048]{3,2,1,0:T(8,128)(2,1)} %bitcast.60) | data formatting | bytes 16777216 | tf_op jit(solution)/shard_map/reshape | solution.py:28
  441.9 74.7 %all-gather.47.cloned.1.call-done = bf16[2048,2048]{1,0:T(8,128)(2,1)} async-done(((bf16[512,2048]{1,0:T(8,128)(2,1)}), bf16[2048,2048]{1,0:T(8,128)(2,1)}) %all-gather.47.cloned.1.call-update) | async-done | bytes 8388624 | tf_op jit(solution)/shard_map/all_gather | solution.py:26
  516.6 8.3 %copy.8 = bf16[4,2,256,2048]{3,2,0,1:T(8,128)(2,1)} copy(bf16[4,2,256,2048]{3,2,1,0:T(8,128)(2,1)} %bitcast.61) | data formatting | bytes 16777216 | tf_op jit(solution)/shard_map/reshape | solution.py:28
  524.9 59.6 %all-gather.25.cloned.1.call-done = bf16[24576,256]{1,0:T(8,128)(2,1)} async-done(((bf16[3072,256]{1,0:T(8,128)(2,1)}), bf16[24576,256]{1,0:T(8,128)(2,1)}) %all-gather.25.cloned.1.call-update) | async-done | bytes 12582928 | tf_op jit(solution)/shard_map/all_gather | solution.py:25
  584.5 30.9 %convolution_bitcast_fusion = f32[3072,2048]{1,0:T(8,128)S(1)} fusion(bf16[8,3072,256]{2,1,0:T(8,128)(2,1)} %bitcast.68, bf16[8,256,2048]{2,1,0:T(8,128)(2,1)} %bitcast.67), kind=kOutput, calls=%fused_computation.2 | convolution fusion | flops 25769803776 | bytes 46137344 | tf_op jit(solution)/shard_map/qrjc,jqcm->rm/dot_general | solution.py:30
  615.5 8.3 %copy-done.2 = f32[3072,2048]{1,0:T(8,128)} copy-done((f32[3072,2048]{1,0:T(8,128)}, f32[3072,2048]{1,0:T(8,128)S(1)}, u32[]{:S(2)}) %copy-start.2) | copy-done | bytes 25165848
  625.4 17.0 %all-gather.29.cloned.1.call-done = bf16[20480,256]{1,0:T(8,128)(2,1)} async-done(((bf16[2560,256]{1,0:T(8,128)(2,1)}), bf16[20480,256]{1,0:T(8,128)(2,1)}) %all-gather.29.cloned.1.call-update) | async-done | bytes 10485776 | tf_op jit(solution)/shard_map/all_gather | solution.py:25
  642.4 30.3 %slice_add_fusion = f32[2560,2048]{1,0:T(8,128)} fusion(f32[3072,2048]{1,0:T(8,128)} %copy-done.2, bf16[8,2560,256]{2,1,0:T(8,128)(2,1)} %bitcast.69, bf16[8,256,2048]{2,1,0:T(8,128)(2,1)} %bitcast.66), kind=kOutput, calls=%fused_computation | convolution fusion | flops 21480079360 | bytes 60817408 | tf_op jit(solution)/shard_map/qrjc,jqcm->rm/dot_general | solution.py:30
  672.7 3.8 fusion.3
  676.6 14.8 %all-gather.33.cloned.1.call-done = bf16[16384,256]{1,0:T(8,128)(2,1)} async-done(((bf16[2048,256]{1,0:T(8,128)(2,1)}), bf16[16384,256]{1,0:T(8,128)(2,1)}) %all-gather.33.cloned.1.call-update) | async-done | bytes 8388624 | tf_op jit(solution)/shard_map/all_gather | solution.py:25
  691.3 26.2 %slice_add_fusion.1 = f32[2048,2048]{1,0:T(8,128)} fusion(f32[2560,2048]{1,0:T(8,128)} %slice_add_fusion, bf16[8,2048,256]{2,1,0:T(8,128)(2,1)} %bitcast.70, bf16[8,256,2048]{2,1,0:T(8,128)(2,1)} %bitcast.65), kind=kOutput, calls=%fused_computation.1 | convolution fusion | flops 17184063488 | bytes 50331648 | tf_op jit(solution)/shard_map/qrjc,jqcm->rm/dot_general | solution.py:30
  717.5 13.6 %all-gather.37.cloned.1.call-done = bf16[12288,256]{1,0:T(8,128)(2,1)} async-done(((bf16[1536,256]{1,0:T(8,128)(2,1)}), bf16[12288,256]{1,0:T(8,128)(2,1)}) %all-gather.37.cloned.1.call-update) | async-done | bytes 6291472 | tf_op jit(solution)/shard_map/all_gather | solution.py:25
  731.1 18.2 %slice_add_fusion.2 = f32[1536,2048]{1,0:T(8,128)S(1)} fusion(f32[2048,2048]{1,0:T(8,128)} %slice_add_fusion.1, bf16[8,1536,256]{2,1,0:T(8,128)(2,1)} %bitcast.71, bf16[8,256,2048]{2,1,0:T(8,128)(2,1)} %bitcast.64), kind=kOutput, calls=%fused_computation.3 | convolution fusion | flops 12888047616 | bytes 39845888 | tf_op jit(solution)/shard_map/qrjc,jqcm->rm/dot_general | solution.py:30
  749.3 7.0 fusion.4
  757.9 4.2 all-gather.41.cloned.1.call-done
  762.2 13.9 %slice_add_fusion.3 = f32[1024,2048]{1,0:T(8,128)S(1)} fusion(f32[1536,2048]{1,0:T(8,128)} %copy-done.1, bf16[8,1024,256]{2,1,0:T(8,128)(2,1)} %bitcast.72, bf16[8,256,2048]{2,1,0:T(8,128)(2,1)} %bitcast.63), kind=kOutput, calls=%fused_computation.4 | convolution fusion | flops 8592031744 | bytes 29360128 | tf_op jit(solution)/shard_map/qrjc,jqcm->rm/dot_general | solution.py:30
  776.1 3.3 copy-done
  781.1 5.1 all-gather.45.cloned.1.call-done
  786.1 11.0 %fusion.1 = bf16[3072,2048]{1,0:T(8,128)(2,1)} fusion(bf16[3072,2048]{1,0:T(8,128)(2,1)} %fusion.6, bf16[8,512,256]{2,1,0:T(8,128)(2,1)} %bitcast.73, bf16[8,256,2048]{2,1,0:T(8,128)(2,1)} %bitcast.62, f32[1024,2048]{1,0:T(8,128)} %copy-done), kind=kOutput, calls=%fused_computation.12 | convolution fusion | flops 4297064448 | bytes 16777216 | tf_op jit(solution)/shard_map/qrjc,jqcm->rm/dot_general | solution.py:30
  (34 shorter events, 14.8 us)
Async XLA Ops:
  6.5 94.0 %all-gather.27.cloned.1.call-start = ((), (), s32[]{:S(2)}) async-start(), calls=%async_computation.1 | async-start | bytes 10485760 | tf_op jit(solution)/shard_map/all_gather | solution.py:26
  15.8 168.0 %all-gather.31.cloned.1.call-start = ((), (), s32[]{:S(2)}) async-start(), calls=%async_computation.3 | async-start | bytes 10485760 | tf_op jit(solution)/shard_map/all_gather | solution.py:26
  16.7 250.5 %all-gather.35.cloned.1.call-start = ((), (), s32[]{:S(2)}) async-start(), calls=%async_computation.5 | async-start | bytes 10485760 | tf_op jit(solution)/shard_map/all_gather | solution.py:26
  17.4 332.8 %all-gather.39.cloned.1.call-start = ((), (), s32[]{:S(2)}) async-start(), calls=%async_computation.7 | async-start | bytes 10485760 | tf_op jit(solution)/shard_map/all_gather | solution.py:26
  18.1 415.4 %all-gather.43.cloned.1.call-start = ((), (), s32[]{:S(2)}) async-start(), calls=%async_computation.9 | async-start | bytes 10485760 | tf_op jit(solution)/shard_map/all_gather | solution.py:26
  18.7 497.9 %all-gather.47.cloned.1.call-start = ((), (), s32[]{:S(2)}) async-start(), calls=%async_computation.11 | async-start | bytes 10485760 | tf_op jit(solution)/shard_map/all_gather | solution.py:26
  19.4 565.2 %all-gather.25.cloned.1.call-start = ((), (), s32[]{:S(2)}) async-start(), calls=%async_computation | async-start | bytes 14155776 | tf_op jit(solution)/shard_map/all_gather | solution.py:25
  22.2 620.2 %all-gather.29.cloned.1.call-start = ((), (), s32[]{:S(2)}) async-start(), calls=%async_computation.2 | async-start | bytes 11796480 | tf_op jit(solution)/shard_map/all_gather | solution.py:25
  24.8 666.5 %all-gather.33.cloned.1.call-start = ((), (), s32[]{:S(2)}) async-start(), calls=%async_computation.4 | async-start | bytes 9437184 | tf_op jit(solution)/shard_map/all_gather | solution.py:25
  27.2 703.9 %all-gather.37.cloned.1.call-start = ((), (), s32[]{:S(2)}) async-start(), calls=%async_computation.6 | async-start | bytes 7077888 | tf_op jit(solution)/shard_map/all_gather | solution.py:25
  29.5 732.7 %all-gather.41.cloned.1.call-start = ((), (), s32[]{:S(2)}) async-start(), calls=%async_computation.8 | async-start | bytes 4718592 | tf_op jit(solution)/shard_map/all_gather | solution.py:25
  31.5 754.6 %all-gather.45.cloned.1.call-start = ((), (), s32[]{:S(2)}) async-start(), calls=%async_computation.10 | async-start | bytes 2359296 | tf_op jit(solution)/shard_map/all_gather | solution.py:25
  615.5 8.3 %copy-start.2 = (f32[3072,2048]{1,0:T(8,128)}, f32[3072,2048]{1,0:T(8,128)S(1)}, u32[]{:S(2)}) copy-start(f32[3072,2048]{1,0:T(8,128)S(1)} %convolution_bitcast_fusion) | copy-start | bytes 75497472
  749.3 7.0 copy-start.1
  776.1 3.3 copy-start
Sparse Core Ops, SparseCore 0:
  16.0 84.4 all-gather.26
  102.1 81.6 all-gather.30
  185.4 81.6 all-gather.34
  268.6 81.6 all-gather.38
  351.7 81.6 all-gather.42
  434.9 81.6 all-gather.46
  518.2 66.2 all-gather.24
  586.1 56.2 all-gather.28
  644.1 47.2 all-gather.32
  692.8 38.2 all-gather.36
  732.7 29.4 all-gather.40
  763.7 22.4 all-gather.44
where the time goes:
time: 805 us; the launch traced here: 804 us
  waiting for transfers between devices  559 us (69%)
  matrix products  131 us (16%)
  local copies, waits for them, and re-layouts  99.8 us (12%)
  between operations  13.7 us (2%)
    all_gather x6, waiting for transfers between devices, local_trmm(): b_all = lax.all_gather(b_panel, 'row')  441 us
    dot_general x6, matrix products, local_trmm(): jnp.einsum('qrjc,jqcm->rm', l_all, b_all, preferred_element_type=jnp.floa...  131 us
    all_gather x6, waiting for transfers between devices, local_trmm(): l_all = lax.all_gather(l_panel, 'col')  114 us
    reshape x6, local copies, waits for them, and re-layouts, local_trmm(): b_all.reshape(grid_rows, span // grid_rows, BLOCK_SIZE, cols_loc)  50.2 us
    unnamed x11, local copies, waits for them, and re-layouts  27.3 us
  transfers between devices with their start and end apart: 12, of which 12 were waited for; matrix products, arithmetic and copies ran while one was open for 25% of the time, Pallas kernels for 0%

commit v1 on v0

v1 whole, which is shorter than its diff:
```python
import functools

import jax
import jax.numpy as jnp
from jax import lax
from jax.experimental import pallas as pl
from jax.experimental.pallas import tpu as pltpu
from jax.sharding import PartitionSpec as P

BLOCK_SIZE = 256
TILE = 256
NUM_WIDE = 4
MESH = pl.DeviceIdType.MESH

PANELS = ((0, 0), (0, 1), (0, 2), (0, 3), (1, 2), (1, 3), (0, 4), (1, 4), (0, 5), (1, 5))
PART_B = ((-1, 0), (-1, 0), (0, 1), (1, 0), (1, 1), (2, 1), (3, 1), (4, 1), (6, 1), (8, 1))
PART_C = ((0, 0), (0, 1), (1, 1), (2, 0), (3, 0), (4, 0), (5, 1), (7, 0), (9, 1), (10, 0))


def kernel(bs, tile, tri, rhs, out, bg, lg, lbuf, bbuf, acc, obuf, lsem, bsem, osem,
           b_send, b_recv, w_send, w_recv, t_send, t_recv, x_send, x_recv, d_send, d_recv,
           o_send, o_recv):
    groups = rhs.shape[0] // bs
    half = rhs.shape[1] // 2
    grid_rows = bg.shape[0]
    grid_cols = lg.shape[1]
    y = lax.axis_index("row")
    q = lax.axis_index("col")
    mate = y + 1 - 2 * lax.rem(y, 2)
    peer = grid_rows - 1 - y
    far = grid_rows - 1 - mate
    mine = lax.rem((y + 1) // 2 + 1, 2)
    q_up = lax.rem(q + 2, grid_cols)
    q_down = lax.rem(q + grid_cols - 2, grid_cols)
    q_far = lax.rem(q + grid_cols // 2, grid_cols)
    q_twin = q + 1 - 2 * lax.rem(q, 2)

    def send(src, dst, ss, rs, **where):
        return pltpu.make_async_remote_copy(src_ref=src, dst_ref=dst, send_sem=ss, recv_sem=rs,
                                            device_id=where, device_id_type=MESH)

    def landed(ref, sem):
        pltpu.make_async_copy(ref, ref, sem).wait()

    def cols_of(side):
        return pl.ds(pl.multiple_of(side * half, half), half)

    def rows_of(j, count=1):
        return pl.ds(pl.multiple_of(j * bs, bs), count * bs)

    def b_copy(kind, j, wide):
        sems = (w_send, w_recv) if wide else (b_send, b_recv)
        side = (mine if kind == 0 else 1 - mine) if wide else (1 - mine if kind == 0 else mine)
        part = (rows_of(j), cols_of(side))
        src = bg.at[(mate, *part)] if kind == 2 else rhs.at[part]
        dst = bg.at[(mate if kind == 2 else y, *part)]
        return send(src, dst, sems[0].at[kind, j], sems[1].at[kind, j], row=mate if kind == 0 else peer)

    def b_landed(kind, j, wide):
        owner = (mate, peer, far)[kind]
        sem = w_recv if wide else b_recv
        landed(bg.at[owner, rows_of(j), cols_of(1 - mine if wide else mine)], sem.at[kind, j])

    def both(j, act):
        act(False)
        if isinstance(j, int):
            if j < NUM_WIDE:
                act(True)
        else:
            @pl.when(j < NUM_WIDE)
            def _():
                act(True)

    def panel(m):
        return rows_of(2 * m, 2), pl.ds(0, (m + 1) * bs)

    def tri_copy(m):
        t = m - NUM_WIDE // 2
        part = panel(m)
        return send(tri.at[part], lg.at[(1, q, *part)], t_send.at[t], t_recv.at[t], row=mate)

    def l_own(n):
        cls, m = PANELS[n]
        return lg.at[(1, q, *panel(m))] if cls else tri.at[panel(m)]

    def l_copy(n, way):
        cls, m = PANELS[n]
        sems = x_send.at[n, way], x_recv.at[n, way]
        if way < 2:
            return send(l_own(n), lg.at[(cls, q, *panel(m))], *sems, col=q_down if way else q_up)
        owner = q_up if way == 3 else q_down
        part = lg.at[cls, owner, rows_of(2 * m + way - 2), pl.ds(0, (m + 1) * bs)]
        return send(part, part, *sems, col=q_down if way == 3 else q_up)

    def twin_copy(n, way):
        cls, m = PANELS[n]
        owner = (q, q_down, q_up, q_far)[way]
        dst = lg.at[(cls, owner, *panel(m))]
        src = l_own(n) if way == 0 else dst
        return send(src, dst, d_send.at[n, way], d_recv.at[n, way], col=q_twin)

    def part_a(n):
        cls, m = PANELS[n]
        if cls:
            landed(lg.at[(1, q, *panel(m))], t_recv.at[m - NUM_WIDE // 2])
        for way in range(2):
            l_copy(n, way).start()
        twin_copy(n, 0).start()

    def part_b(n):
        cls, m = PANELS[n]
        for way, owner in enumerate((q_down, q_up)):
            landed(lg.at[(cls, owner, *panel(m))], x_recv.at[n, way])
            l_copy(n, 2 + way).start()
        for way in range(2):
            twin_copy(n, 1 + way).start()
        if n + 2 < len(PANELS):
            part_a(n + 2)

    def part_c(n):
        cls, m = PANELS[n]
        for way in range(2):
            half_panel = lg.at[cls, q_far, rows_of(2 * m + way), pl.ds(0, (m + 1) * bs)]
            landed(half_panel, x_recv.at[n, 2 + way])
        twin_copy(n, 3).start()

    def part_d(n):
        cls, m = PANELS[n]
        for way, owner in enumerate((q, q_down, q_up, q_far)):
            twin = owner + 1 - 2 * lax.rem(owner, 2)
            landed(lg.at[(cls, twin, *panel(m))], d_recv.at[n, way])

    def events(j, pos, lo, hi):
        for n in range(len(PANELS)):
            for spots, part in ((PART_C, part_c), (PART_B, part_b)):
                if spots[n][1] == pos and lo <= spots[n][0] < hi:
                    pl.when(j == spots[n][0])(functools.partial(part, n))
        if pos == 0:
            for n, (_, m) in enumerate(PANELS):
                if lo <= 2 * m < hi:
                    pl.when(j == 2 * m)(functools.partial(part_d, n))

    def fetch_l(j, g, slot, wide):
        spot = rows_of(j), rows_of(g // 2)
        for p in range(4):
            owner = 4 * lax.rem(g, 2) + p
            dst = lbuf.at[slot, pl.ds(0, bs), pl.ds(p * bs, bs)]

            @pl.when(owner == q)
            def _():
                pltpu.make_async_copy(tri.at[spot], dst, lsem.at[slot]).start()

            @pl.when(owner != q)
            def _():
                pltpu.make_async_copy(lg.at[(0, owner, *spot)], dst, lsem.at[slot]).start()

            if not wide:
                dst = lbuf.at[slot, pl.ds(bs, bs), pl.ds(p * bs, bs)]
                pltpu.make_async_copy(lg.at[(1, owner, *spot)], dst, lsem.at[slot]).start()

    def fetch_b(g, slot, wide):
        for side in range(2 if wide else 1):
            spot = rows_of(g), cols_of(side if wide else mine)
            for p in range(4):
                dst = bbuf.at[slot, side, pl.ds(p * bs, bs), :]

                @pl.when(p == y)
                def _():
                    pltpu.make_async_copy(rhs.at[spot], dst, bsem.at[slot]).start()

                @pl.when(p != y)
                def _():
                    pltpu.make_async_copy(bg.at[(p, *spot)], dst, bsem.at[slot]).start()

    def fetched(slot, wide):
        l_part = lbuf.at[slot, pl.ds(0, bs)] if wide else lbuf.at[slot]
        b_part = bbuf.at[slot] if wide else bbuf.at[slot, 0]
        landed(l_part, lsem.at[slot])
        landed(b_part, bsem.at[slot])

    tiles = half // tile

    def multiply(slot, wide):
        if wide:
            @pl.loop(0, 2 * tiles)
            def _(n):
                side = n // tiles
                cols = pl.ds(pl.multiple_of(lax.rem(n, tiles) * tile, tile), tile)
                rows = rows_of(side)
                acc[rows, cols] += jnp.dot(lbuf[slot, pl.ds(0, bs), :], bbuf[slot, side, :, cols],
                                           preferred_element_type=jnp.float32)
        else:
            @pl.loop(0, tiles)
            def _(n):
                cols = pl.ds(pl.multiple_of(n * tile, tile), tile)
                acc[:, cols] += jnp.dot(lbuf[slot], bbuf[slot, 0, :, cols],
                                        preferred_element_type=jnp.float32)

    def out_copy(j, side):
        return pltpu.make_async_copy(obuf.at[j, pl.ds(side * bs, bs)], out.at[rows_of(j), cols_of(side)],
                                     osem.at[j])

    def own_copy(j):
        return pltpu.make_async_copy(obuf.at[j, pl.ds(0, bs)], out.at[rows_of(j), cols_of(mine)], osem.at[j])

    def mate_copy(j):
        return send(obuf.at[j, pl.ds(bs, bs)], out.at[rows_of(j), cols_of(mine)], o_send.at[j], o_recv.at[j],
                    row=mate)

    def own_block(j):
        both(j, lambda wide: b_copy(1, j, wide).start())
        both(j, lambda wide: b_copy(0, j, wide).start())

    def stage(j, wide, lo, hi):
        for w in ((False, True) if wide else (False,)):
            b_landed(0, j, w)
            b_copy(2, j, w).start()
        if wide:
            for m in range(NUM_WIDE):
                pl.when(j == m)(lambda m=m: tri_copy(m + NUM_WIDE // 2).start())

        @pl.when(j + 2 < groups)
        def _():
            own_block(j + 2)

        events(j, 0, lo, hi)
        acc[...] = jnp.zeros_like(acc)

        @pl.when(j > 0)
        def _():
            fetch_l(j, 0, 0, wide)
            fetch_b(0, 0, wide)

        @pl.loop(0, j)
        def _(g):
            slot = lax.rem(g, 2)
            fetched(slot, wide)
            fetch_l(j, g + 1, 1 - slot, wide)

            @pl.when(g + 1 < j)
            def _():
                fetch_b(g + 1, 1 - slot, wide)

            multiply(slot, wide)

        events(j, 1, lo, hi)
        last = lax.rem(j, 2)

        @pl.when(j == 0)
        def _():
            fetch_l(j, j, last, wide)

        for w in ((False, True) if wide else (False,)):
            b_landed(1, j, w)
            b_landed(2, j, w)
        fetch_b(j, last, wide)
        fetched(last, wide)
        multiply(last, wide)

        @pl.loop(0, tiles)
        def _(n):
            cols = pl.ds(pl.multiple_of(n * tile, tile), tile)
            obuf[j, :, cols] = acc[:, cols].astype(obuf.dtype)

        if wide:
            out_copy(j, 0).start()
            out_copy(j, 1).start()
        else:
            mate_copy(j).start()
            own_copy(j).start()

    barrier = pltpu.get_barrier_semaphore()
    for where in ({"row": mate}, {"row": peer}, {"col": q_up}, {"col": q_down}, {"col": q_twin}):
        pl.semaphore_signal(barrier, inc=1, device_id=where, device_id_type=MESH)
    pl.semaphore_wait(barrier, 5)

    own_block(0)
    part_a(0)
    own_block(1)
    part_a(1)
    for n in range(len(PANELS)):
        if PART_B[n][0] < 0:
            part_b(n)

    @pl.loop(0, NUM_WIDE)
    def _(j):
        stage(j, True, 0, NUM_WIDE)

    @pl.loop(NUM_WIDE, groups)
    def _(j):
        stage(j, False, NUM_WIDE, groups)

    @pl.loop(0, NUM_WIDE)
    def _(j):
        landed(obuf.at[j], osem.at[j])
        for kind in range(3):
            b_copy(kind, j, True).wait_send()

    @pl.loop(NUM_WIDE, groups)
    def _(j):
        own_copy(j).wait()
        mate_copy(j).wait_send()
        landed(out.at[rows_of(j), cols_of(1 - mine)], o_recv.at[j])

    @pl.loop(0, groups)
    def _(j):
        for kind in range(3):
            b_copy(kind, j, False).wait_send()

    for m in range(NUM_WIDE):
        tri_copy(m + NUM_WIDE // 2).wait_send()
    for n in range(len(PANELS)):
        for way in range(4):
            l_copy(n, way).wait_send()
            twin_copy(n, way).wait_send()


def solution(mesh):
    grid_rows = mesh.shape["row"]
    grid_cols = mesh.shape["col"]
    bs = BLOCK_SIZE

    def local_trmm(tri_loc, rhs_loc):
        rows_loc, cols_loc = rhs_loc.shape
        groups = rows_loc // bs
        half = cols_loc // 2
        dtype = rhs_loc.dtype
        any_spec = pl.BlockSpec(memory_space=pl.ANY)
        dma = pltpu.SemaphoreType.DMA
        panels = len(PANELS)
        res = pl.pallas_call(
            functools.partial(kernel, bs, min(TILE, half)),
            out_shape=[
                jax.ShapeDtypeStruct((rows_loc, cols_loc), dtype),
                jax.ShapeDtypeStruct((grid_rows, rows_loc, cols_loc), dtype),
                jax.ShapeDtypeStruct((2, grid_cols, *tri_loc.shape), dtype),
            ],
            in_specs=[any_spec] * 2,
            out_specs=[any_spec] * 3,
            scratch_shapes=[
                pltpu.VMEM((2, 2 * bs, 4 * bs), dtype),
                pltpu.VMEM((2, 2, 4 * bs, half), dtype),
                pltpu.VMEM((2 * bs, half), jnp.float32),
                pltpu.VMEM((groups, 2 * bs, half), dtype),
                dma((2,)), dma((2,)), dma((groups,)),
                dma((3, groups)), dma((3, groups)),
                dma((3, NUM_WIDE)), dma((3, NUM_WIDE)),
                dma((NUM_WIDE,)), dma((NUM_WIDE,)),
                dma((panels, 4)), dma((panels, 4)),
                dma((panels, 4)), dma((panels, 4)),
                dma((groups,)), dma((groups,)),
            ],
            compiler_params=pltpu.CompilerParams(
                collective_id=0, has_side_effects=True, vmem_limit_bytes=48 * 1024 * 1024),
        )(tri_loc, rhs_loc)
        return res[0]

    part_spec = P(("batch", "row"), "col")
    return jax.shard_map(local_trmm, mesh=mesh, in_specs=(part_spec, part_spec), out_specs=part_spec, check_vma=False)
```

time: 805 us -> 426 us (0.53)
  waiting for transfers between devices: 559 us -> 0 us
  Pallas kernels: 0 us -> 413 us
  matrix products: 131 us -> 0 us
  local copies, waits for them, and re-layouts: 99.8 us -> 10.7 us
  between operations: 13.7 us -> 0.01 us
    all_gather x12 -> x0, waiting for transfers between devices: 556 us -> none  [the longest x6 441 us: local_trmm(): b_all = lax.all_gather(b_panel, 'row')]
    pallas_call x0 -> x1, Pallas kernels: none -> 413 us  [local_trmm(): pl.pallas_call(functools.partial(kernel, bs, min(TILE, half)), out_shape=...]
    dot_general x6 -> x0, matrix products: 131 us -> none  [local_trmm(): jnp.einsum('qrjc,jqcm->rm', l_all, b_all, preferred_element_type=jnp.floa...]
    reshape x6 -> x0, local copies, waits for them, and re-layouts: 50.2 us -> none  [local_trmm(): b_all.reshape(grid_rows, span // grid_rows, BLOCK_SIZE, cols_loc)]
    slice x7 -> x0, local copies, waits for them, and re-layouts: 22.3 us -> none  [the longest x6 13.1 us: local_trmm(): tri_loc[step * row_group:, step * col_group:(step + 1) * col_group]]
    unnamed x11 -> x1, local copies, waits for them, and re-layouts: 27.3 us -> 10.7 us
  transfers between devices with their start and end apart: 12 -> 0, of which waited for: 12 -> 0; matrix products, arithmetic and copies ran while one was open for 25% -> 0% of each run, Pallas kernels for 0% -> 0%
where the time goes in v1:
time: 426 us; the launch traced here: 424 us
  Pallas kernels  413 us (97%)
  local copies, waits for them, and re-layouts  10.7 us (3%)
    pallas_call x1, Pallas kernels, local_trmm(): pl.pallas_call(functools.partial(kernel, bs, min(TILE, half)), out_shape=...  413 us
    unnamed x1, local copies, waits for them, and re-layouts  10.7 us

profile of v1, /device:TPU:97, one launch (start us, length us, event | category | flops | bytes accessed | tf_op | source)
XLA Modules:
  0.0 424.1 jit_solution(15627135938548210988)
XLA Ops:
  0.0 413.4 %shard_map.28 = (bf16[3072,2048]{1,0:T(8,128)(2,1)}, bf16[4,3072,2048]{2,1,0:T(8,128)(2,1)}, bf16[2,8,3072,1536]{3,2,1,0:T(8,128)(2,1)}) custom-call(bf16[3072,1536]{1,0:T(8,128)(2,1)} %tri.1, bf16[3072,2048]{1,0:T(8,128)(2,1)} %rhs.1), custom_call_target="tpu_custom_call" | custom-call | tf_op jit(solution)/shard_map/pallas_call | solution.py:331
  413.4 10.7 %copy.4 = bf16[3072,2048]{1,0:T(8,128)(2,1)} copy(bf16[3072,2048]{1,0:T(8,128)(2,1)} %get-tuple-element.6) | data formatting | bytes 25165824

commit v2 on v0

v2 whole, which is shorter than its diff:
```python
import functools

import jax
import jax.numpy as jnp
from jax import lax
from jax.experimental import pallas as pl
from jax.experimental.pallas import tpu as pltpu
from jax.sharding import PartitionSpec as P

BLOCK_SIZE = 256
TILE = 256
NUM_WIDE = 4
MESH = pl.DeviceIdType.MESH

PANELS = (
    (0, 0, 2), (0, 2, 2), (0, 4, 2), (0, 6, 2), (1, 4, 2), (1, 6, 2), (0, 8, 2),
    (1, 8, 2), (0, 10, 1), (1, 10, 1), (0, 11, 1), (1, 11, 1),
)

SCHEDULE = {
    (-1, 0): ("a3", "p1", "m0", "a0", "m9", "f0", "a2",),
    (0, 0): ("b0", "a1", "m1", "p0", "c0",),
    (0, 1): ("b3", "m2", "f1", "t4", "a6",),
    (1, 0): ("t5", "p2",),
    (1, 1): ("b2",),
    (2, 0): ("b1", "a4", "f2", "c1", "m5", "b6",),
    (2, 1): ("a5", "p3", "m4", "c2", "m3",),
    (3, 0): ("a8", "t7", "f4", "c6", "f3", "m6", "c3",),
    (3, 1): ("f5", "b4", "b5", "t9", "p4",),
    (4, 0): ("p5", "a7", "c4",),
    (4, 1): ("c5", "b8", "m7", "m8",),
    (5, 0): ("p6",),
    (5, 1): ("f6",),
    (6, 0): ("b7", "a9", "p7",),
    (6, 1): ("f7", "t11", "f8",),
    (7, 0): ("a10", "c7", "p8",),
    (8, 0): ("p9", "b9",),
    (8, 1): ("c8", "f9", "a11", "m10",),
    (9, 0): ("c9", "p10", "b10", "m11",),
    (10, 0): ("b11", "f10",),
    (10, 1): ("c11", "c10", "p11", "f11",),
}


def kernel(bs, tile, tri, rhs, out, bg, lg, lbuf, bbuf, acc, obuf, lsem, bsem,
           b_send, b_recv, t_send, t_recv, x_send, x_recv, d_send, d_recv, o_send, o_recv):
    groups = rhs.shape[0] // bs
    last = groups - 1
    half = rhs.shape[1] // 2
    quarter = half // 2
    grid_rows = bg.shape[0]
    grid_cols = lg.shape[1]
    y = lax.axis_index("row")
    q = lax.axis_index("col")
    mate = y + 1 - 2 * lax.rem(y, 2)
    peer = grid_rows - 1 - y
    far = grid_rows - 1 - mate
    mine = lax.rem((y + 1) // 2 + 1, 2)
    q_up = lax.rem(q + 2, grid_cols)
    q_down = lax.rem(q + grid_cols - 2, grid_cols)
    q_far = lax.rem(q + grid_cols // 2, grid_cols)
    q_twin = q + 1 - 2 * lax.rem(q, 2)

    def send(src, dst, ss, rs, **where):
        return pltpu.make_async_remote_copy(src_ref=src, dst_ref=dst, send_sem=ss, recv_sem=rs,
                                            device_id=where, device_id_type=MESH)

    def landed(ref, sem):
        pltpu.make_async_copy(ref, ref, sem).wait()

    def rows_of(j, count=1):
        return pl.ds(pl.multiple_of(j * bs, bs), count * bs)

    def cols_of(side, first=0, width=half):
        return pl.ds(pl.multiple_of(side * half + first, width), width)

    def pieces(j):
        return 2 if j < NUM_WIDE or j == last else 1

    def piece_of(j, part):
        index = 2 * j + part if j < NUM_WIDE else NUM_WIDE + j + part
        if j == last:
            return index, False, part * quarter, quarter
        return index, part == 1, 0, half

    def b_copy(kind, j, part):
        index, other, first, width = piece_of(j, part)
        side = (mine if other else 1 - mine) if kind == 0 else (1 - mine if other else mine)
        spot = (rows_of(j), cols_of(side, first, width))
        src = bg.at[(mate, *spot)] if kind == 2 else rhs.at[spot]
        dst = bg.at[(mate if kind == 2 else y, *spot)]
        return send(src, dst, b_send.at[kind, index], b_recv.at[kind, index], row=mate if kind == 0 else peer)

    def b_landed(kind, rows, cols, index):
        landed(bg.at[(mate, peer, far)[kind], rows, cols], b_recv.at[kind, index])

    def own_b(kind, j):
        for part in range(pieces(j)):
            b_copy(kind, j, part).start()

    def relay_b(j):
        for part in range(pieces(j)):
            index, other, first, width = piece_of(j, part)
            b_landed(0, rows_of(j), cols_of(1 - mine if other else mine, first, width), index)
            b_copy(2, j, part).start()

    def panel(n):
        _, first, count = PANELS[n]
        return rows_of(first, count), pl.ds(0, ((first + count - 1) // 2 + 1) * bs)

    def half_panel(n, part):
        _, first, count = PANELS[n]
        rows = count * bs // 2
        start = pl.multiple_of(first * bs + part * rows, rows)
        return pl.ds(start, rows), pl.ds(0, ((first + count - 1) // 2 + 1) * bs)

    def tri_copy(n):
        return send(tri.at[panel(n)], lg.at[(1, q, *panel(n))], t_send.at[n], t_recv.at[n], row=mate)

    def l_own(n):
        return lg.at[(1, q, *panel(n))] if PANELS[n][0] else tri.at[panel(n)]

    def l_copy(n, way):
        cls = PANELS[n][0]
        sems = x_send.at[n, way], x_recv.at[n, way]
        where = q_up if way in (0, 2) else q_down
        if way < 2:
            return send(l_own(n), lg.at[(cls, q, *panel(n))], *sems, col=where)
        part = lg.at[(cls, q_down if way == 2 else q_up, *half_panel(n, way - 2))]
        return send(part, part, *sems, col=where)

    def twin_copy(n, way):
        cls = PANELS[n][0]
        dst = lg.at[(cls, (q, q_down, q_up, q_far)[way], *panel(n))]
        return send(l_own(n) if way == 0 else dst, dst, d_send.at[n, way], d_recv.at[n, way], col=q_twin)

    def part_a(n):
        if PANELS[n][0]:
            landed(l_own(n), t_recv.at[n])
        for way in range(2):
            l_copy(n, way).start()
        twin_copy(n, 0).start()

    def part_b(n):
        for way, owner in enumerate((q_down, q_up)):
            landed(lg.at[(PANELS[n][0], owner, *panel(n))], x_recv.at[n, way])
            l_copy(n, 2 + way).start()
        for way in range(2):
            twin_copy(n, 1 + way).start()

    def part_c(n):
        for way in range(2):
            landed(lg.at[(PANELS[n][0], q_far, *half_panel(n, way))], x_recv.at[n, 2 + way])
        twin_copy(n, 3).start()

    def part_d(n):
        for way, owner in enumerate((q, q_down, q_up, q_far)):
            twin = owner + 1 - 2 * lax.rem(owner, 2)
            landed(lg.at[(PANELS[n][0], twin, *panel(n))], d_recv.at[n, way])

    steps = {
        "p": functools.partial(own_b, 1), "m": functools.partial(own_b, 0), "f": relay_b,
        "t": lambda n: tri_copy(n).start(), "a": part_a, "b": part_b, "c": part_c,
    }

    def play(group, pos):
        for text in SCHEDULE.get((group, pos), ()):
            steps[text[0]](int(text[1:]))
        if pos == 0:
            for n, (_, first, _) in enumerate(PANELS):
                if first == group:
                    part_d(n)

    def events(j, pos, lo, hi):
        for group in range(lo, hi):
            if SCHEDULE.get((group, pos)) or (pos == 0 and any(p[1] == group for p in PANELS)):
                pl.when(j == group)(functools.partial(play, group, pos))

    def fetch_l(j, g, slot, wide):
        spot = rows_of(j), rows_of(g // 2)
        for p in range(4):
            owner = 4 * lax.rem(g, 2) + p
            dst = lbuf.at[slot, pl.ds(0, bs), pl.ds(p * bs, bs)]

            @pl.when(owner == q)
            def _():
                pltpu.make_async_copy(tri.at[spot], dst, lsem.at[slot]).start()

            @pl.when(owner != q)
            def _():
                pltpu.make_async_copy(lg.at[(0, owner, *spot)], dst, lsem.at[slot]).start()

            if not wide:
                dst = lbuf.at[slot, pl.ds(bs, bs), pl.ds(p * bs, bs)]
                pltpu.make_async_copy(lg.at[(1, owner, *spot)], dst, lsem.at[slot]).start()

    def fetch_block(owner, g, slot, wide, first=0, width=half):
        for side in range(2 if wide else 1):
            spot = rows_of(g), cols_of(side if wide else mine, first, width)
            dst = bbuf.at[slot, side, rows_of(owner), pl.ds(first, width)]

            @pl.when(owner == y)
            def _():
                pltpu.make_async_copy(rhs.at[spot], dst, bsem.at[slot]).start()

            @pl.when(owner != y)
            def _():
                pltpu.make_async_copy(bg.at[(owner, *spot)], dst, bsem.at[slot]).start()

    def fetch_b(g, slot, wide):
        for p in range(4):
            fetch_block(p, g, slot, wide)

    def l_fetched(slot, wide):
        landed(lbuf.at[slot, pl.ds(0, bs)] if wide else lbuf.at[slot], lsem.at[slot])

    def b_fetched(slot, wide):
        landed(bbuf.at[slot] if wide else bbuf.at[slot, 0], bsem.at[slot])

    tiles = half // tile

    def product(slot, n, wide):
        if wide:
            side, cols = n // tiles, pl.ds(pl.multiple_of(lax.rem(n, tiles) * tile, tile), tile)
            rows = rows_of(side)
            left = lbuf[slot, pl.ds(0, bs), :]
        else:
            side, cols = 0, pl.ds(pl.multiple_of(n * tile, tile), tile)
            rows = pl.ds(0, 2 * bs)
            left = lbuf[slot]
        term = jnp.dot(left, bbuf[slot, side, :, cols], preferred_element_type=jnp.float32)
        return rows, cols, acc[rows, cols] + term

    def multiply(slot, wide):
        @pl.loop(0, 2 * tiles if wide else tiles)
        def _(n):
            rows, cols, total = product(slot, n, wide)
            acc[rows, cols] = total

    def finish(j, slot, wide, lo=0, hi=tiles):
        @pl.loop(lo, 2 * tiles if wide else hi)
        def _(n):
            _, _, total = product(slot, n, wide)
            total = total.astype(out.dtype)
            if wide:
                out[rows_of(j), pl.ds(pl.multiple_of(n * tile, tile), tile)] = total
            else:
                cols = pl.ds(pl.multiple_of(n * tile, tile), tile)
                obuf[rows_of(j - NUM_WIDE), cols] = total[bs:]
                cols = pl.ds(pl.multiple_of(mine * half + n * tile, tile), tile)
                out[rows_of(j), cols] = total[:bs]

    def mate_copy(j, index, first=0, width=half):
        return send(obuf.at[rows_of(j - NUM_WIDE), pl.ds(first, width)],
                    out.at[rows_of(j), cols_of(mine, first, width)],
                    o_send.at[index], o_recv.at[index], row=mate)

    def older_terms(j, wide):
        acc[...] = jnp.zeros_like(acc)
        fetch_l(j, 0, 0, wide)
        if not wide:
            fetch_b(0, 0, wide)
        else:
            pl.when(j > 0)(lambda: fetch_b(0, 0, wide))

        @pl.loop(0, j)
        def _(g):
            slot = lax.rem(g, 2)
            l_fetched(slot, wide)
            b_fetched(slot, wide)
            fetch_l(j, g + 1, 1 - slot, wide)

            @pl.when(g + 1 < j)
            def _():
                fetch_b(g + 1, 1 - slot, wide)

            multiply(slot, wide)

    def stage(j, wide, lo, hi):
        events(j, 0, lo, hi)
        older_terms(j, wide)
        events(j, 1, lo, hi)
        slot = lax.rem(j, 2)
        fetch_block(y, j, slot, wide)
        fetch_block(mate, j, slot, wide)
        for kind, owner in ((1, peer), (2, far)):
            if wide:
                b_landed(kind, rows_of(j), cols_of(mine), 2 * j)
                b_landed(kind, rows_of(j), cols_of(1 - mine), 2 * j + 1)
            else:
                b_landed(kind, rows_of(j), cols_of(mine), NUM_WIDE + j)
            fetch_block(owner, j, slot, wide)
        l_fetched(slot, wide)
        b_fetched(slot, wide)
        finish(j, slot, wide)
        if not wide:
            mate_copy(j, j - NUM_WIDE).start()

    barrier = pltpu.get_barrier_semaphore()
    for where in ({"row": mate}, {"row": peer}, {"col": q_up}, {"col": q_down}, {"col": q_twin}):
        pl.semaphore_signal(barrier, inc=1, device_id=where, device_id_type=MESH)
    pl.semaphore_wait(barrier, 5)

    play(-1, 0)

    @pl.loop(0, NUM_WIDE)
    def _(j):
        stage(j, True, 0, NUM_WIDE)

    @pl.loop(NUM_WIDE, last)
    def _(j):
        stage(j, False, NUM_WIDE, last)

    play(last, 0)
    older_terms(last, False)
    play(last, 1)
    slot = last % 2
    l_fetched(slot, False)
    for part in range(2):
        index, _, first, width = piece_of(last, part)
        fetch_block(y, last, slot, False, first, width)
        fetch_block(mate, last, slot, False, first, width)
        for kind, owner in ((1, peer), (2, far)):
            b_landed(kind, rows_of(last), cols_of(mine, first, width), index)
            fetch_block(owner, last, slot, False, first, width)
        landed(bbuf.at[slot, 0, :, pl.ds(first, width)], bsem.at[slot])
        finish(last, slot, False, part * tiles // 2, (part + 1) * tiles // 2)
        mate_copy(last, last - NUM_WIDE + part, first, width).start()

    for j in range(groups):
        for kind in range(3):
            for part in range(pieces(j)):
                b_copy(kind, j, part).wait_send()
    for n in range(len(PANELS)):
        if PANELS[n][0]:
            tri_copy(n).wait_send()
        for way in range(4):
            l_copy(n, way).wait_send()
            twin_copy(n, way).wait_send()

    @pl.loop(NUM_WIDE, last)
    def _(j):
        mate_copy(j, j - NUM_WIDE).wait_send()
        landed(out.at[rows_of(j), cols_of(1 - mine)], o_recv.at[j - NUM_WIDE])

    for part in range(2):
        index, _, first, width = piece_of(last, part)
        mate_copy(last, last - NUM_WIDE + part, first, width).wait_send()
        landed(out.at[rows_of(last), cols_of(1 - mine, first, width)], o_recv.at[last - NUM_WIDE + part])


def emit(parts, src, dst, sem):
    rows = src.shape[0] // parts

    def copy(n):
        spot = pl.ds(n * rows, rows)
        return pltpu.make_async_copy(src.at[spot], dst.at[spot], sem.at[n])

    for n in range(parts):
        copy(n).start()
    for n in range(parts):
        copy(n).wait()


def solution(mesh):
    grid_rows = mesh.shape["row"]
    grid_cols = mesh.shape["col"]
    bs = BLOCK_SIZE

    def local_trmm(tri_loc, rhs_loc):
        rows_loc, cols_loc = rhs_loc.shape
        groups = rows_loc // bs
        half = cols_loc // 2
        dtype = rhs_loc.dtype
        any_spec = pl.BlockSpec(memory_space=pl.ANY)
        vmem_spec = pl.BlockSpec(memory_space=pltpu.VMEM)
        dma = pltpu.SemaphoreType.DMA
        panels = len(PANELS)
        in_vmem, _, _ = pl.pallas_call(
            functools.partial(kernel, bs, min(TILE, half)),
            out_shape=[
                pltpu.VMEM((rows_loc, cols_loc), dtype),
                jax.ShapeDtypeStruct((grid_rows, rows_loc, cols_loc), dtype),
                jax.ShapeDtypeStruct((2, grid_cols, *tri_loc.shape), dtype),
            ],
            in_specs=[any_spec] * 2,
            out_specs=[vmem_spec, any_spec, any_spec],
            scratch_shapes=[
                pltpu.VMEM((2, 2 * bs, 4 * bs), dtype),
                pltpu.VMEM((2, 2, 4 * bs, half), dtype),
                pltpu.VMEM((2 * bs, half), jnp.float32),
                pltpu.VMEM(((groups - NUM_WIDE) * bs, half), dtype),
                dma((2,)), dma((2,)),
                dma((3, groups + NUM_WIDE + 1)), dma((3, groups + NUM_WIDE + 1)),
                dma((panels,)), dma((panels,)),
                dma((panels, 4)), dma((panels, 4)),
                dma((panels, 4)), dma((panels, 4)),
                dma((groups - NUM_WIDE + 1,)), dma((groups - NUM_WIDE + 1,)),
            ],
            compiler_params=pltpu.CompilerParams(
                collective_id=0, has_side_effects=True, vmem_limit_bytes=36 * 1024 * 1024),
        )(tri_loc, rhs_loc)
        return pl.pallas_call(
            functools.partial(emit, groups),
            out_shape=jax.ShapeDtypeStruct((rows_loc, cols_loc), dtype),
            in_specs=[vmem_spec],
            out_specs=any_spec,
            scratch_shapes=[dma((groups,))],
            compiler_params=pltpu.CompilerParams(vmem_limit_bytes=1024 * 1024),
        )(in_vmem)

    part_spec = P(("batch", "row"), "col")
    return jax.shard_map(local_trmm, mesh=mesh, in_specs=(part_spec, part_spec), out_specs=part_spec, check_vma=False)
```

time: 805 us -> 399 us (0.50)
  waiting for transfers between devices: 559 us -> 0 us
  Pallas kernels: 0 us -> 397 us
  matrix products: 131 us -> 0 us
  local copies, waits for them, and re-layouts: 99.8 us -> 0 us
  between operations: 13.7 us -> 0.01 us
    all_gather x12 -> x0, waiting for transfers between devices: 556 us -> none  [the longest x6 441 us: local_trmm(): b_all = lax.all_gather(b_panel, 'row')]
    pallas_call x0 -> x2, Pallas kernels: none -> 397 us  [the longest x1 393 us: local_trmm(): pl.pallas_call(functools.partial(kernel, bs, min(TILE, half)), out_shape=...]
    dot_general x6 -> x0, matrix products: 131 us -> none  [local_trmm(): jnp.einsum('qrjc,jqcm->rm', l_all, b_all, preferred_element_type=jnp.floa...]
    reshape x6 -> x0, local copies, waits for them, and re-layouts: 50.2 us -> none  [local_trmm(): b_all.reshape(grid_rows, span // grid_rows, BLOCK_SIZE, cols_loc)]
    unnamed x11 -> x0, local copies, waits for them, and re-layouts: 27.3 us -> none
    slice x7 -> x0, local copies, waits for them, and re-layouts: 22.3 us -> none  [the longest x6 13.1 us: local_trmm(): tri_loc[step * row_group:, step * col_group:(step + 1) * col_group]]
  transfers between devices with their start and end apart: 12 -> 0, of which waited for: 12 -> 0; matrix products, arithmetic and copies ran while one was open for 25% -> 0% of each run, Pallas kernels for 0% -> 0%
where the time goes in v2:
time: 399 us; the launch traced here: 397 us
  Pallas kernels  397 us (99%)
    pallas_call x1, Pallas kernels, local_trmm(): pl.pallas_call(functools.partial(kernel, bs, min(TILE, half)), out_shape=...  393 us

profile of v2, /device:TPU:97, one launch (start us, length us, event | category | flops | bytes accessed | tf_op | source)
XLA Modules:
  0.0 397.3 jit_solution(4360098864924174854)
XLA Ops:
  0.0 392.6 %shard_map.28 = (bf16[3072,2048]{1,0:T(8,128)(2,1)S(1)}, bf16[4,3072,2048]{2,1,0:T(8,128)(2,1)}, bf16[2,8,3072,1536]{3,2,1,0:T(8,128)(2,1)}) custom-call(bf16[3072,1536]{1,0:T(8,128)(2,1)} %tri.1, bf16[3072,2048]{1,0:T(8,128)(2,1)} %rhs.1), custom_call_target="tpu_custom_call" | custom-call | tf_op jit(solution)/shard_map/pallas_call | solution.py:379
  392.7 4.7 %shard_map.29 = bf16[3072,2048]{1,0:T(8,128)(2,1)} custom-call(bf16[3072,2048]{1,0:T(8,128)(2,1)S(1)} %get-tuple-element.6.src), custom_call_target="tpu_custom_call" | custom-call | tf_op jit(solution)/shard_map/pallas_call | solution.py:403

commit v3 on v2

--- a/solution.py
+++ b/solution.py
@@ -10,6 +10,7 @@
 BLOCK_SIZE = 256
 TILE = 256
 NUM_WIDE = 4
+SLOTS = 4
 MESH = pl.DeviceIdType.MESH
 
 PANELS = (
@@ -18,27 +19,28 @@
 )
 
 SCHEDULE = {
-    (-1, 0): ("a3", "p1", "m0", "a0", "m9", "f0", "a2",),
-    (0, 0): ("b0", "a1", "m1", "p0", "c0",),
-    (0, 1): ("b3", "m2", "f1", "t4", "a6",),
-    (1, 0): ("t5", "p2",),
-    (1, 1): ("b2",),
-    (2, 0): ("b1", "a4", "f2", "c1", "m5", "b6",),
-    (2, 1): ("a5", "p3", "m4", "c2", "m3",),
-    (3, 0): ("a8", "t7", "f4", "c6", "f3", "m6", "c3",),
-    (3, 1): ("f5", "b4", "b5", "t9", "p4",),
-    (4, 0): ("p5", "a7", "c4",),
-    (4, 1): ("c5", "b8", "m7", "m8",),
-    (5, 0): ("p6",),
-    (5, 1): ("f6",),
-    (6, 0): ("b7", "a9", "p7",),
-    (6, 1): ("f7", "t11", "f8",),
-    (7, 0): ("a10", "c7", "p8",),
-    (8, 0): ("p9", "b9",),
-    (8, 1): ("c8", "f9", "a11", "m10",),
-    (9, 0): ("c9", "p10", "b10", "m11",),
-    (10, 0): ("b11", "f10",),
-    (10, 1): ("c11", "c10", "p11", "f11",),
+    (-1, 0): ("m0", "p5", "p0", "a0", "a1", "b0", "m1", "a6",),
+    (0, 0): ("c0",),
+    (0, 1): ("t4", "a2", "f0", "f1", "m9",),
+    (1, 0): ("b6", "b2", "m2",),
+    (1, 1): ("t5", "a3", "p1", "f2", "b1",),
+    (2, 0): ("c2", "b3", "t7", "c1", "p2", "p4", "a4",),
+    (2, 1): ("a5", "m4", "b4", "p3", "m3",),
+    (3, 0): ("a7",),
+    (3, 1): ("c4", "m6", "b5", "c3", "m5", "m8", "f3", "f4", "t9",),
+    (4, 0): ("a8", "b7", "p6",),
+    (4, 1): ("m7", "f5",),
+    (5, 0): ("f6", "c5",),
+    (5, 1): ("t11", "c6",),
+    (6, 0): ("a9", "a10", "f7",),
+    (6, 1): ("p7", "p8", "b8", "f8",),
+    (7, 1): ("b9", "m10", "c7",),
+    (8, 0): ("p9",),
+    (8, 1): ("f9", "c8", "a11", "m11",),
+    (9, 0): ("p10", "c9",),
+    (9, 1): ("b10",),
+    (10, 0): ("f10", "b11",),
+    (10, 1): ("c10", "p11", "f11", "c11",),
 }
 
 
@@ -256,31 +258,34 @@
                     o_send.at[index], o_recv.at[index], row=mate)
 
     def older_terms(j, wide):
+        def fetch(g):
+            slot = lax.rem(g, SLOTS)
+
+            @pl.when(g <= j)
+            def _():
+                fetch_l(j, g, slot, wide)
+
+            @pl.when(g < j)
+            def _():
+                fetch_b(g, slot, wide)
+
+        for g in range(SLOTS - 1):
+            fetch(g)
         acc[...] = jnp.zeros_like(acc)
-        fetch_l(j, 0, 0, wide)
-        if not wide:
-            fetch_b(0, 0, wide)
-        else:
-            pl.when(j > 0)(lambda: fetch_b(0, 0, wide))
 
         @pl.loop(0, j)
         def _(g):
-            slot = lax.rem(g, 2)
+            slot = lax.rem(g, SLOTS)
             l_fetched(slot, wide)
             b_fetched(slot, wide)
-            fetch_l(j, g + 1, 1 - slot, wide)
-
-            @pl.when(g + 1 < j)
-            def _():
-                fetch_b(g + 1, 1 - slot, wide)
-
+            fetch(g + SLOTS - 1)
             multiply(slot, wide)
 
     def stage(j, wide, lo, hi):
         events(j, 0, lo, hi)
         older_terms(j, wide)
         events(j, 1, lo, hi)
-        slot = lax.rem(j, 2)
+        slot = lax.rem(j, SLOTS)
         fetch_block(y, j, slot, wide)
         fetch_block(mate, j, slot, wide)
         for kind, owner in ((1, peer), (2, far)):
@@ -314,7 +319,7 @@
     play(last, 0)
     older_terms(last, False)
     play(last, 1)
-    slot = last % 2
+    slot = last % SLOTS
     l_fetched(slot, False)
     for part in range(2):
         index, _, first, width = piece_of(last, part)
@@ -386,11 +391,11 @@
             in_specs=[any_spec] * 2,
             out_specs=[vmem_spec, any_spec, any_spec],
             scratch_shapes=[
-                pltpu.VMEM((2, 2 * bs, 4 * bs), dtype),
-                pltpu.VMEM((2, 2, 4 * bs, half), dtype),
+                pltpu.VMEM((SLOTS, 2 * bs, 4 * bs), dtype),
+                pltpu.VMEM((SLOTS, 2, 4 * bs, half), dtype),
                 pltpu.VMEM((2 * bs, half), jnp.float32),
                 pltpu.VMEM(((groups - NUM_WIDE) * bs, half), dtype),
-                dma((2,)), dma((2,)),
+                dma((SLOTS,)), dma((SLOTS,)),
                 dma((3, groups + NUM_WIDE + 1)), dma((3, groups + NUM_WIDE + 1)),
                 dma((panels,)), dma((panels,)),
                 dma((panels, 4)), dma((panels, 4)),
@@ -398,7 +403,7 @@
                 dma((groups - NUM_WIDE + 1,)), dma((groups - NUM_WIDE + 1,)),
             ],
             compiler_params=pltpu.CompilerParams(
-                collective_id=0, has_side_effects=True, vmem_limit_bytes=36 * 1024 * 1024),
+                collective_id=0, has_side_effects=True, vmem_limit_bytes=44 * 1024 * 1024),
         )(tri_loc, rhs_loc)
         return pl.pallas_call(
             functools.partial(emit, groups),

time: 399 us -> 401 us (level)
  no operation moved by 1% of the time
where the time goes in v3:
time: 401 us; the launch traced here: 400 us
  Pallas kernels  400 us (100%)
    pallas_call x1, Pallas kernels, local_trmm(): pl.pallas_call(functools.partial(kernel, bs, min(TILE, half)), out_shape=...  396 us

profile of v3, /device:TPU:97, one launch (start us, length us, event | category | flops | bytes accessed | tf_op | source)
XLA Modules:
  0.0 400.4 jit_solution(4911328526047823235)
XLA Ops:
  0.0 395.7 %shard_map.28 = (bf16[3072,2048]{1,0:T(8,128)(2,1)S(1)}, bf16[4,3072,2048]{2,1,0:T(8,128)(2,1)}, bf16[2,8,3072,1536]{3,2,1,0:T(8,128)(2,1)}) custom-call(bf16[3072,1536]{1,0:T(8,128)(2,1)} %tri.1, bf16[3072,2048]{1,0:T(8,128)(2,1)} %rhs.1), custom_call_target="tpu_custom_call" | custom-call | tf_op jit(solution)/shard_map/pallas_call | solution.py:384
  395.7 4.7 %shard_map.29 = bf16[3072,2048]{1,0:T(8,128)(2,1)} custom-call(bf16[3072,2048]{1,0:T(8,128)(2,1)S(1)} %get-tuple-element.6.src), custom_call_target="tpu_custom_call" | custom-call | tf_op jit(solution)/shard_map/pallas_call | solution.py:408

commit v4 on v3

--- a/solution.py
+++ b/solution.py
@@ -19,28 +19,24 @@
 )
 
 SCHEDULE = {
-    (-1, 0): ("m0", "p5", "p0", "a0", "a1", "b0", "m1", "a6",),
-    (0, 0): ("c0",),
-    (0, 1): ("t4", "a2", "f0", "f1", "m9",),
-    (1, 0): ("b6", "b2", "m2",),
-    (1, 1): ("t5", "a3", "p1", "f2", "b1",),
-    (2, 0): ("c2", "b3", "t7", "c1", "p2", "p4", "a4",),
-    (2, 1): ("a5", "m4", "b4", "p3", "m3",),
-    (3, 0): ("a7",),
-    (3, 1): ("c4", "m6", "b5", "c3", "m5", "m8", "f3", "f4", "t9",),
-    (4, 0): ("a8", "b7", "p6",),
-    (4, 1): ("m7", "f5",),
-    (5, 0): ("f6", "c5",),
-    (5, 1): ("t11", "c6",),
-    (6, 0): ("a9", "a10", "f7",),
-    (6, 1): ("p7", "p8", "b8", "f8",),
-    (7, 1): ("b9", "m10", "c7",),
-    (8, 0): ("p9",),
-    (8, 1): ("f9", "c8", "a11", "m11",),
-    (9, 0): ("p10", "c9",),
-    (9, 1): ("b10",),
-    (10, 0): ("f10", "b11",),
-    (10, 1): ("c10", "p11", "f11", "c11",),
+    (-1, 0): ("t5", "m0", "p0", "t4", "a6", "p1", "a0", "a8",),
+    (0, 0): ("b0", "a2", "p3", "f0", "c0",),
+    (0, 1): ("a1", "m1", "b6", "m2", "t7", "b1", "p2", "m3",),
+    (1, 0): ("p4", "a4", "b2", "a5", "f1", "c2", "m4",),
+    (1, 1): ("f2", "a3",),
+    (2, 0): ("m5", "b5", "f3", "c1", "p6", "m7", "t9",),
+    (2, 1): ("b4", "f4", "b3", "c5", "m8",),
+    (3, 0): ("c4", "m6", "f5", "a7", "p5",),
+    (4, 1): ("b8", "m9",),
+    (5, 0): ("f6", "t11", "c6", "p7", "b7", "c3",),
+    (6, 0): ("f7", "a9",),
+    (6, 1): ("p8", "f8",),
+    (7, 0): ("a10", "m10", "c8", "c7",),
+    (8, 0): ("f9", "b9",),
+    (9, 0): ("p9", "a11", "c9",),
+    (9, 1): ("m11", "f10", "b10",),
+    (10, 0): ("b11", "p10",),
+    (10, 1): ("p11", "c11", "c10", "f11",),
 }
 
 

time: 401 us -> 403 us (level)
  no operation moved by 1% of the time
where the time goes in v4:
time: 403 us; the launch traced here: 402 us
  Pallas kernels  402 us (100%)
    pallas_call x1, Pallas kernels, local_trmm(): pl.pallas_call(functools.partial(kernel, bs, min(TILE, half)), out_shape=...  397 us

profile of v4, /device:TPU:97, one launch (start us, length us, event | category | flops | bytes accessed | tf_op | source)
XLA Modules:
  0.0 402.2 jit_solution(9658640521959231691)
XLA Ops:
  0.0 397.5 %shard_map.28 = (bf16[3072,2048]{1,0:T(8,128)(2,1)S(1)}, bf16[4,3072,2048]{2,1,0:T(8,128)(2,1)}, bf16[2,8,3072,1536]{3,2,1,0:T(8,128)(2,1)}) custom-call(bf16[3072,1536]{1,0:T(8,128)(2,1)} %tri.1, bf16[3072,2048]{1,0:T(8,128)(2,1)} %rhs.1), custom_call_target="tpu_custom_call" | custom-call | tf_op jit(solution)/shard_map/pallas_call | solution.py:380
  397.5 4.7 %shard_map.29 = bf16[3072,2048]{1,0:T(8,128)(2,1)} custom-call(bf16[3072,2048]{1,0:T(8,128)(2,1)S(1)} %get-tuple-element.6.src), custom_call_target="tpu_custom_call" | custom-call | tf_op jit(solution)/shard_map/pallas_call | solution.py:404
